TPU v7x, 256 devices: a 8x8x2 block of a 8x8x16 slice. The times are simulated.
256 devices in a mesh: grp: 2 (over z), row: 16 (over x, core), col: 8 (over y).
Axes of the slice: x: 8, y: 8, z: 2, core: 2. Of those that a mesh axis runs over, the one named last changes fastest.
The devices are a block of a 8x8x16 slice.
Arguments:
- perturbation: bfloat16 [4, 12000, 12000], P('grp', 'row', 'col'), parts along dimension 0, may hold values from -96 to 96
- occ_coeffs: bfloat16 [12000, 2000], P('row', 'col'), may hold values from -0.0546875 to 0.0546875
- vir_coeffs: bfloat16 [12000, 512], P('col', 'row'), may hold values from -0.0546875 to 0.0546875
- occ_energies: float32 [2000], replicated, may hold values from -1 to -0.1
- vir_energies: float32 [512], replicated, may hold values from 0.1 to 1.5
Outputs:
- density_response: bfloat16 [4, 12000, 12000], P('grp', 'row', 'col'), parts along dimension 0
There are 2 independent parts, one for each index of `grp`. A program takes and returns all parts, laid end to end along the dimension named above; an argument that names none is the same for every part. Nothing has to cross between parts.
All inputs are finite; a program needn't handle non-finite values.
Results may differ from a plain program's by a relative error of at most 0.0098.
Values may be sent and summed in bfloat16 or wider, within the bound.
No kernel may reach another device: no remote copies, remote signals or barrier semaphores. Data moves between devices by JAX's collectives and lax.ppermute only.
A program may use at most 64 MiB of HBM per device.

v0:
```python
import jax
import jax.numpy as jnp
from jax import lax
from jax.sharding import Mesh
from jax.sharding import PartitionSpec as P

ROW = ("row_0", "row_1")


def joined_along(pieces, dim):
    pieces = jnp.moveaxis(pieces, 0, dim)
    dims = pieces.shape
    return pieces.reshape(*dims[:dim], dims[dim] * dims[dim + 1], *dims[dim + 2 :])


def sent_to_all(shard, axis):
    copies = jnp.broadcast_to(shard, (lax.axis_size(axis), *shard.shape))
    return lax.all_to_all(copies, axis, split_axis=0, concat_axis=0, tiled=True)


def collect(shard, axis, dim):
    return joined_along(sent_to_all(shard, axis), dim)


def cut_along(shard, dim, count):
    before, after = (shard.shape[:dim], shard.shape[dim + 1 :])
    return jnp.moveaxis(shard.reshape(*before, count, -1, *after), dim, 0)


def summed_on_arrival(shard, axis, dim):
    count = lax.axis_size(axis)
    pieces = lax.all_to_all(cut_along(shard, dim, count), axis, 0, 0, tiled=True)
    return jnp.sum(pieces.astype(jnp.float32), axis=0)


def padded_to(lines, count):
    spare = -len(lines) % count
    return jnp.pad(lines, [(0, spare)] + [(0, 0)] * (lines.ndim - 1))


def reduced_to_own(pieces, axes, order):
    inside = pieces.shape[1:]
    pieces = pieces.reshape(*(lax.axis_size(a) for a in axes), *inside)
    pieces = jnp.moveaxis(pieces, order, range(len(axes))).reshape(-1, *inside)
    for k in order:
        pieces = lax.psum_scatter(pieces, axes[k], scatter_dimension=0, tiled=True)
    return pieces[0]


def stacked_from(shard, axes, order):
    pieces = shard[None]
    for k in order:
        pieces = lax.all_gather(pieces, axes[k], axis=0, tiled=True)
    carried = [lax.axis_size(axes[k]) for k in reversed(order)]
    pieces = pieces.reshape(*carried, *shard.shape)
    turned = sorted(range(len(order)), key=lambda place: order[len(order) - 1 - place])
    return pieces.transpose(*turned, *range(len(order), pieces.ndim)).reshape(-1, *shard.shape)


def sum_by_parts(shard, axes, order):
    count, lines = (lax.axis_size(axes), shard.reshape(-1, *shard.shape[1:][-1:]))
    pieces = padded_to(lines, count).reshape(count, -1, *lines.shape[1:])
    own = reduced_to_own(pieces, axes, order)
    whole = stacked_from(own, axes, order[::-1]).reshape(-1, *lines.shape[1:])
    return whole[: len(lines)].reshape(shard.shape)


def per_device(perturbation, occ_coeffs, vir_coeffs, occ_energies, vir_energies):
    occ_rows = lax.all_gather(occ_coeffs, "col", axis=1, tiled=True)
    vir_rows = collect(vir_coeffs, ROW, 1)
    share = vir_rows.shape[1] // lax.axis_size("col")
    image = summed_on_arrival(
        jnp.einsum(
            "pij,jv->vpi", perturbation, vir_rows, preferred_element_type=jnp.float32
        ).astype(jnp.bfloat16),
        "col",
        0,
    )
    partial_value = jnp.einsum(
        "io,vpi->pov", occ_rows.astype(jnp.float32), image, precision=lax.Precision.HIGHEST
    )
    coupling = sum_by_parts(partial_value, ROW, (0, 1))
    offset = lax.axis_index("col") * share
    energies = lax.dynamic_slice_in_dim(vir_energies, offset, share, 0)
    gaps = occ_energies[:, None] - energies[None, :]
    response = (coupling / gaps[None, :, :]).astype(jnp.bfloat16)
    mixed = jnp.einsum(
        "io,pov->piv", occ_rows, response, preferred_element_type=jnp.float32
    ).astype(jnp.bfloat16)
    total = jnp.einsum(
        "piv,jv->pij", collect(mixed, "col", 2), vir_rows, preferred_element_type=jnp.float32
    )
    return total.astype(jnp.bfloat16)


def solution(mesh):
    torus = Mesh(
        mesh.devices.reshape(mesh.shape["grp"], 8, 2, mesh.shape["col"]),
        ("grp", "row_0", "row_1", "col"),
    )
    in_specs = (P("grp", ROW, "col"), P(ROW, "col"), P("col", ROW), P(), P())
    out_specs = P("grp", ROW, "col")
    return jax.shard_map(
        per_device, mesh=torus, in_specs=in_specs, out_specs=out_specs, check_vma=False
    )
```

profile of v0, /device:TPU:516, one launch (start us, length us, event | category | flops | bytes accessed | tf_op | source)
XLA Modules:
  0.0 288.0 jit_solution(6391762949328565553)
XLA Ops:
  6.5 2.2 broadcast_in_dim.4
  8.7 22.8 %all-to-all-start = ((bf16[16,1500,32]{1,2,0:T(8,128)(2,1)}), bf16[16,1500,32]{1,2,0:T(8,128)(2,1)S(1)}, u32[]{:S(2)}, u32[]{:S(2)}) async-start(bf16[16,1500,32]{1,2,0:T(8,128)(2,1)} %broadcast_in_dim.4), calls=%async_computation | async-start | bytes 3145728 | tf_op jit(solution)/shard_map/all_to_all | solution.py:18
  31.5 0.1 all-gather.3.cloned.1.call-start
  31.6 0.7 all-gather.3.cloned.1.call-update
  32.3 35.1 %all-to-all-done = bf16[16,1500,32]{1,2,0:T(8,128)(2,1)S(1)} async-done(((bf16[16,1500,32]{1,2,0:T(8,128)(2,1)}), bf16[16,1500,32]{1,2,0:T(8,128)(2,1)S(1)}, u32[]{:S(2)}, u32[]{:S(2)}) %all-to-all-start) | async-done | bytes 1536032 | tf_op jit(solution)/shard_map/all_to_all | solution.py:18
  67.4 0.0 copy-start
  67.4 1.1 copy-done
  68.6 4.9 %fusion.9 = bf16[512,2,750]{0,2,1:T(8,128)(2,1)S(1)} fusion(bf16[1500,512,1]{0,1,2:T(8,128)(2,1)S(1)} %bitcast.40, bf16[2,750,1500]{2,0,1:T(2,128)(2,1)} %param.5), kind=kOutput, calls=%fused_computation.9 | convolution fusion | flops 2304768000 | bytes 7572000 | tf_op jit(solution)/shard_map/pij,jv->vpi/dot_general | solution.py:73
  73.5 0.7 copy.24
  74.2 1.3 copy.25
  75.5 4.5 %all-to-all-start.1 = ((bf16[8,64,2,750]{3,1,2,0:T(8,128)(2,1)}), bf16[8,64,2,750]{3,1,2,0:T(8,128)(2,1)}, u32[]{:S(2)}, u32[]{:S(2)}) async-start(bf16[8,64,2,750]{3,1,2,0:T(8,128)(2,1)} %copy.25), calls=%async_computation.1 | async-start | bytes 3145728 | tf_op jit(solution)/shard_map/all_to_all | solution.py:32
  80.0 0.1 reduce-scatter.3.cloned.1.call-start
  80.0 2.3 all-gather.3.cloned.1.call-done
  82.3 4.6 %copy.26 = bf16[8,250,750]{1,0,2:T(8,128)(2,1)} copy(bf16[8,250,750]{1,2,0:T(8,128)(2,1)} %all-gather.3.cloned.1.call-done) | data formatting | bytes 6000000 | tf_op jit(solution)/shard_map/all_gather | solution.py:69
  86.9 5.5 %reshape.42 = bf16[2000,750]{0,1:T(8,128)(2,1)S(1)} reshape(bf16[8,250,750]{1,0,2:T(8,128)(2,1)} %copy.26) | data formatting | bytes 6000000
  92.4 28.9 %all-to-all-done.1 = bf16[8,64,2,750]{3,1,2,0:T(8,128)(2,1)} async-done(((bf16[8,64,2,750]{3,1,2,0:T(8,128)(2,1)}), bf16[8,64,2,750]{3,1,2,0:T(8,128)(2,1)}, u32[]{:S(2)}, u32[]{:S(2)}) %all-to-all-start.1) | async-done | bytes 1536032 | tf_op jit(solution)/shard_map/all_to_all | solution.py:32
  121.3 1.7 convert_reduce_fusion
  123.0 1.5 fusion.6
  124.4 1.8 copy.28
  126.2 0.0 copy-start.2
  126.2 3.5 %reshape_reshape_reshape.3 = f32[16,250,64]{1,0,2:T(8,128)} reshape(f32[2,2000,64]{1,0,2:T(2,128)} %copy.28) | data formatting | bytes 2048000 | tf_op jit(solution)/shard_map/reshape;reshape;reshape | solution.py:44
  129.7 2.8 copy.29
  132.5 0.1 reduce-scatter.3.cloned.1.call-update
  132.6 0.1 reduce-scatter.5.cloned.1.call-start
  132.6 0.8 dynamic_slice.3
  133.4 36.3 %reduce-scatter.3.cloned.1.call-done = f32[2,250,64]{1,2,0:T(8,128)} async-done(((f32[16,250,64]{1,2,0:T(8,128)}), f32[2,250,64]{1,2,0:T(8,128)}) %reduce-scatter.3.cloned.1.call-update) | async-done | bytes 128016 | tf_op jit(solution)/shard_map/reduce_scatter | solution.py:46
  169.7 0.1 reduce-scatter.5.cloned.1.call-update
  169.7 0.0 copy-done.2
  169.7 0.9 broadcast_subtract_fusion
  170.7 16.2 %reduce-scatter.5.cloned.1.call-done = f32[1,250,64]{1,2,0:T(8,128)} async-done(((f32[2,250,64]{1,2,0:T(8,128)}), f32[1,250,64]{1,2,0:T(8,128)}) %reduce-scatter.5.cloned.1.call-update) | async-done | bytes 64016 | tf_op jit(solution)/shard_map/reduce_scatter | solution.py:46
  186.9 2.1 all_gather.10
  189.0 28.1 %all_gather.11 = f32[16,250,64]{1,2,0:T(8,128)S(1)} all-gather(f32[2,250,64]{1,2,0:T(8,128)S(1)} %all_gather.10), channel_id=1, replica_groups=mesh['grp'=2,'row_0'=8,'row_1'=2,'col'=8] {'row_0'}, dimensions={0}, use_global_device_ids=true | all-gather | bytes 1152000 | tf_op jit(solution)/shard_map/all_gather | solution.py:53
  217.1 1.6 copy.30
  218.7 3.7 %reshape_reshape_reshape_reshape.3 = f32[2,2000,64]{1,0,2:T(2,128)} reshape(f32[16,250,64]{1,0,2:T(8,128)} %copy.30) | data formatting | bytes 2048000 | tf_op jit(solution)/shard_map/reshape;reshape;reshape;reshape | solution.py:65
  222.4 1.9 divide_convert_fusion
  224.3 1.1 fusion.15
  225.4 0.1 broadcast_in_dim.10
  225.5 0.0 copy-start.1
  225.5 41.8 %all_to_all.15 = bf16[8,2,750,64]{2,3,1,0:T(8,128)(2,1)S(1)} all-to-all(bf16[8,2,750,64]{2,3,1,0:T(8,128)(2,1)S(1)} %broadcast_in_dim.10), channel_id=1, replica_groups=mesh['grp'=2,'row_0'=8,'row_1'=2,'col'=8] {'col'}, dimensions={0} | all-to-all | bytes 3072000 | tf_op jit(solution)/shard_map/all_to_all | solution.py:18
  267.4 0.1 copy.33
  267.5 0.0 copy-done.1
  267.5 4.7 %convolution_convert_fusion = bf16[2,750,1500]{2,1,0:T(8,128)(2,1)} fusion(bf16[2,750,512]{1,2,0:T(8,128)(2,1)S(1)} %bitcast.42, bf16[1500,512,1]{0,1,2:T(8,128)(2,1)S(1)} %bitcast.41), kind=kOutput, calls=%fused_computation.2 | convolution fusion | flops 2306249984 | bytes 7572000 | tf_op jit(solution)/shard_map/piv,jv->pij/dot_general | solution.py:90
  272.2 9.2 %copy.36 = bf16[2,750,1500]{2,0,1:T(2,128)(2,1)} copy(bf16[2,750,1500]{2,1,0:T(8,128)(2,1)} %convolution_convert_fusion) | data formatting | bytes 9000000 | tf_op jit(solution)/shard_map/convert_element_type | solution.py:93
Async XLA Ops:
  8.7 58.7 %all-to-all-start = ((bf16[16,1500,32]{1,2,0:T(8,128)(2,1)}), bf16[16,1500,32]{1,2,0:T(8,128)(2,1)S(1)}, u32[]{:S(2)}, u32[]{:S(2)}) async-start(bf16[16,1500,32]{1,2,0:T(8,128)(2,1)} %broadcast_in_dim.4), calls=%async_computation | async-start | bytes 3145728 | tf_op jit(solution)/shard_map/all_to_all | solution.py:18
  31.5 50.8 %all-gather.3.cloned.1.call-start = ((), (), s32[]{:S(2)}) async-start(), calls=%async_computation.7 | async-start | bytes 3465216 | tf_op jit(solution)/shard_map/all_gather | solution.py:69
  67.4 1.2 copy-start
  75.5 45.8 %all-to-all-start.1 = ((bf16[8,64,2,750]{3,1,2,0:T(8,128)(2,1)}), bf16[8,64,2,750]{3,1,2,0:T(8,128)(2,1)}, u32[]{:S(2)}, u32[]{:S(2)}) async-start(bf16[8,64,2,750]{3,1,2,0:T(8,128)(2,1)} %copy.25), calls=%async_computation.1 | async-start | bytes 3145728 | tf_op jit(solution)/shard_map/all_to_all | solution.py:32
  80.0 89.7 %reduce-scatter.3.cloned.1.call-start = ((), (), s32[]{:S(2)}) async-start(), calls=%async_computation.5 | async-start | bytes 1179648 | tf_op jit(solution)/shard_map/reduce_scatter | solution.py:46
  126.2 43.5 %copy-start.2 = (f32[2000]{0:T(1024)S(1)}, f32[2000]{0:T(1024)}, u32[]{:S(2)}) copy-start(f32[2000]{0:T(1024)} %param.8) | copy-start | bytes 24004
  132.6 54.3 %reduce-scatter.5.cloned.1.call-start = ((), (), s32[]{:S(2)}) async-start(), calls=%async_computation.6 | async-start | bytes 196608 | tf_op jit(solution)/shard_map/reduce_scatter | solution.py:46
  225.5 42.0 %copy-start.1 = (bf16[16,1500,32]{1,2,0:T(8,128)(2,1)S(1)}, bf16[16,1500,32]{1,2,0:T(8,128)(2,1)}, u32[]{:S(2)}) copy-start(bf16[16,1500,32]{1,2,0:T(8,128)(2,1)} %copy-done) | copy-start | bytes 4608004
Sparse Core Ops, SparseCore 0:
  34.2 48.1 all-gather.2
  132.7 36.9 reduce-scatter.2
  172.1 14.6 reduce-scatter.4
where the time goes:
time: 289 us; the launch traced here: 288 us
  waiting for transfers between devices  120 us (42%)
  blocking collectives  72.1 us (25%)
  local copies, waits for them, and re-layouts  38.9 us (13%)
  starting transfers between devices  27.4 us (9%)
  between operations  13.2 us (5%)
  matrix products  12.2 us (4%)
  other arithmetic  4.5 us (2%)
    reduce_scatter x2, waiting for transfers between devices, reduced_to_own(): pieces = lax.psum_scatter(pieces, axes[k], scatter_dimension=0, tiled=True)  52.5 us
    all_to_all x1, blocking collectives, sent_to_all(): return lax.all_to_all(copies, axis, split_axis=0, concat_axis=0, tiled=True)  41.8 us
    all_to_all x1, waiting for transfers between devices, sent_to_all(): return lax.all_to_all(copies, axis, split_axis=0, concat_axis=0, tiled=True)  35.1 us
    all_gather x2, blocking collectives, stacked_from(): pieces = lax.all_gather(pieces, axes[k], axis=0, tiled=True)  30.3 us
    all_to_all x1, waiting for transfers between devices, summed_on_arrival(): lax.all_to_all(cut_along(shard, dim, count), axis, 0, 0, tiled=True)  28.9 us
    all_to_all x1, starting transfers between devices, sent_to_all(): return lax.all_to_all(copies, axis, split_axis=0, concat_axis=0, tiled=True)  22.8 us
    convert_element_type x1, local copies, waits for them, and re-layouts, per_device(): return total.astype(jnp.bfloat16)  9.19 us
    unnamed x7, local copies, waits for them, and re-layouts  6.63 us
  transfers between devices with their start and end apart: 5, of which 5 were waited for; matrix products, arithmetic and copies ran while one was open for 6% of the time, Pallas kernels for 0%

commit v1 on v0

--- a/solution.py
+++ b/solution.py
@@ -5,6 +5,13 @@
 from jax.sharding import PartitionSpec as P
 
 ROW = ("row_0", "row_1")
+
+
+def all_by_exchange(x, mesh_axis, along):
+    peers = lax.axis_size(mesh_axis)
+    blocks = jnp.stack([x for _ in range(peers)])
+    blocks = lax.all_to_all(blocks, mesh_axis, split_axis=0, concat_axis=0)
+    return jnp.concatenate(blocks, axis=along)
 
 
 def joined_along(pieces, dim):
@@ -50,7 +57,7 @@
 def stacked_from(shard, axes, order):
     pieces = shard[None]
     for k in order:
-        pieces = lax.all_gather(pieces, axes[k], axis=0, tiled=True)
+        pieces = all_by_exchange(pieces, axes[k], 0)
     carried = [lax.axis_size(axes[k]) for k in reversed(order)]
     pieces = pieces.reshape(*carried, *shard.shape)
     turned = sorted(range(len(order)), key=lambda place: order[len(order) - 1 - place])

time: 289 us -> 310 us (1.073); the launches traced: 288 us -> 304 us
  waiting for transfers between devices: 120 us -> 146 us
  blocking collectives: 72.1 us -> 47.6 us
  starting transfers between devices: 27.4 us -> 34.7 us
  local copies, waits for them, and re-layouts: 38.9 us -> 43.1 us
    all_gather x2 -> x0, blocking collectives: 30.3 us -> none  [stacked_from(): pieces = lax.all_gather(pieces, axes[k], axis=0, tiled=True)]
    all_to_all x0 -> x1, waiting for transfers between devices: none -> 24.9 us  [all_by_exchange(): blocks = lax.all_to_all(blocks, mesh_axis, split_axis=0, concat_axis=0)]
    all_to_all x0 -> x1, starting transfers between devices: none -> 7.26 us  [all_by_exchange(): blocks = lax.all_to_all(blocks, mesh_axis, split_axis=0, concat_axis=0)]
    all_to_all x0 -> x1, blocking collectives: none -> 3.85 us  [all_by_exchange(): blocks = lax.all_to_all(blocks, mesh_axis, split_axis=0, concat_axis=0)]
  transfers between devices with their start and end apart: 5 -> 6, of which waited for: 5 -> 6; matrix products, arithmetic and copies ran while one was open for 6% -> 7% of each run, Pallas kernels for 0% -> 0%
where the time goes in v1:
time: 310 us; the launch traced here: 304 us
  waiting for transfers between devices  146 us (47%)
  blocking collectives  47.6 us (15%)
  local copies, waits for them, and re-layouts  43.1 us (14%)
  starting transfers between devices  34.7 us (11%)
  matrix products  13.3 us (4%)
  between operations  13.2 us (4%)
  other arithmetic  5.43 us (2%)
    reduce_scatter x2, waiting for transfers between devices, reduced_to_own(): pieces = lax.psum_scatter(pieces, axes[k], scatter_dimension=0, tiled=True)  54.2 us
    all_to_all x1, blocking collectives, sent_to_all(): return lax.all_to_all(copies, axis, split_axis=0, concat_axis=0, tiled=True)  43.8 us
    all_to_all x1, waiting for transfers between devices, sent_to_all(): return lax.all_to_all(copies, axis, split_axis=0, concat_axis=0, tiled=True)  35.1 us
    all_to_all x1, waiting for transfers between devices, summed_on_arrival(): lax.all_to_all(cut_along(shard, dim, count), axis, 0, 0, tiled=True)  31.1 us
    all_to_all x1, waiting for transfers between devices, all_by_exchange(): blocks = lax.all_to_all(blocks, mesh_axis, split_axis=0, concat_axis=0)  24.9 us
    all_to_all x1, starting transfers between devices, sent_to_all(): return lax.all_to_all(copies, axis, split_axis=0, concat_axis=0, tiled=True)  22.8 us
    convert_element_type x1, local copies, waits for them, and re-layouts, per_device(): return total.astype(jnp.bfloat16)  9.19 us
    all_to_all x1, starting transfers between devices, all_by_exchange(): blocks = lax.all_to_all(blocks, mesh_axis, split_axis=0, concat_axis=0)  7.26 us
  transfers between devices with their start and end apart: 6, of which 6 were waited for; matrix products, arithmetic and copies ran while one was open for 7% of the time, Pallas kernels for 0%

profile of v1, /device:TPU:516, one launch (start us, length us, event | category | flops | bytes accessed | tf_op | source)
XLA Modules:
  0.0 303.6 jit_solution(12539879394825256082)
XLA Ops:
  6.5 2.2 broadcast_in_dim.4
  8.7 22.8 %all-to-all-start = ((bf16[16,1500,32]{1,2,0:T(8,128)(2,1)}), bf16[16,1500,32]{1,2,0:T(8,128)(2,1)S(1)}, u32[]{:S(2)}, u32[]{:S(2)}) async-start(bf16[16,1500,32]{1,2,0:T(8,128)(2,1)} %broadcast_in_dim.4), calls=%async_computation | async-start | bytes 3145728 | tf_op jit(solution)/shard_map/all_to_all | solution.py:25
  31.5 0.1 all-gather.3.cloned.1.call-start
  31.6 0.7 all-gather.3.cloned.1.call-update
  32.3 35.1 %all-to-all-done = bf16[16,1500,32]{1,2,0:T(8,128)(2,1)S(1)} async-done(((bf16[16,1500,32]{1,2,0:T(8,128)(2,1)}), bf16[16,1500,32]{1,2,0:T(8,128)(2,1)S(1)}, u32[]{:S(2)}, u32[]{:S(2)}) %all-to-all-start) | async-done | bytes 1536032 | tf_op jit(solution)/shard_map/all_to_all | solution.py:25
  67.4 0.0 copy-start
  67.4 1.2 copy-done
  68.6 6.1 %fusion.9 = bf16[512,2,750]{0,2,1:T(8,128)(2,1)} fusion(bf16[1500,512,1]{0,1,2:T(8,128)(2,1)S(1)} %bitcast.42, bf16[2,750,1500]{2,0,1:T(2,128)(2,1)} %param.5), kind=kOutput, calls=%fused_computation.9 | convolution fusion | flops 2304768000 | bytes 7572000 | tf_op jit(solution)/shard_map/pij,jv->vpi/dot_general | solution.py:80
  74.7 1.7 copy.24
  76.4 1.3 copy.25
  77.7 4.5 %all-to-all-start.1 = ((bf16[8,64,2,750]{3,1,2,0:T(8,128)(2,1)}), bf16[8,64,2,750]{3,1,2,0:T(8,128)(2,1)}, u32[]{:S(2)}, u32[]{:S(2)}) async-start(bf16[8,64,2,750]{3,1,2,0:T(8,128)(2,1)} %copy.25), calls=%async_computation.1 | async-start | bytes 3145728 | tf_op jit(solution)/shard_map/all_to_all | solution.py:39
  82.2 0.1 reduce-scatter.3.cloned.1.call-start
  82.2 0.1 all-gather.3.cloned.1.call-done
  82.3 4.6 %copy.26 = bf16[8,250,750]{1,0,2:T(8,128)(2,1)} copy(bf16[8,250,750]{1,2,0:T(8,128)(2,1)} %all-gather.3.cloned.1.call-done) | data formatting | bytes 6000000 | tf_op jit(solution)/shard_map/all_gather | solution.py:76
  86.9 5.5 %reshape.44 = bf16[2000,750]{0,1:T(8,128)(2,1)S(1)} reshape(bf16[8,250,750]{1,0,2:T(8,128)(2,1)} %copy.26) | data formatting | bytes 6000000
  92.4 31.1 %all-to-all-done.1 = bf16[8,64,2,750]{3,1,2,0:T(8,128)(2,1)} async-done(((bf16[8,64,2,750]{3,1,2,0:T(8,128)(2,1)}), bf16[8,64,2,750]{3,1,2,0:T(8,128)(2,1)}, u32[]{:S(2)}, u32[]{:S(2)}) %all-to-all-start.1) | async-done | bytes 1536032 | tf_op jit(solution)/shard_map/all_to_all | solution.py:39
  123.5 1.7 convert_reduce_fusion
  125.2 1.5 fusion.6
  126.6 1.8 copy.28
  128.4 3.5 %reshape_reshape_reshape.3 = f32[16,250,64]{1,0,2:T(8,128)} reshape(f32[2,2000,64]{1,0,2:T(2,128)} %copy.28) | data formatting | bytes 2048000 | tf_op jit(solution)/shard_map/reshape;reshape;reshape | solution.py:51
  131.9 2.8 copy.29
  134.7 0.0 copy-start.2
  134.7 0.1 reduce-scatter.3.cloned.1.call-update
  134.7 0.1 reduce-scatter.5.cloned.1.call-start
  134.8 37.0 %reduce-scatter.3.cloned.1.call-done = f32[2,250,64]{1,2,0:T(8,128)} async-done(((f32[16,250,64]{1,2,0:T(8,128)}), f32[2,250,64]{1,2,0:T(8,128)}) %reduce-scatter.3.cloned.1.call-update) | async-done | bytes 128016 | tf_op jit(solution)/shard_map/reduce_scatter | solution.py:53
  171.8 0.1 reduce-scatter.5.cloned.1.call-update
  171.9 17.1 %reduce-scatter.5.cloned.1.call-done = f32[1,250,64]{1,2,0:T(8,128)} async-done(((f32[2,250,64]{1,2,0:T(8,128)}), f32[1,250,64]{1,2,0:T(8,128)}) %reduce-scatter.5.cloned.1.call-update) | async-done | bytes 64016 | tf_op jit(solution)/shard_map/reduce_scatter | solution.py:53
  189.0 0.9 pad_maximum_fusion
  190.0 3.9 %all_to_all.25 = f32[2,1,250,64]{2,3,1,0:T(8,128)S(1)} all-to-all(f32[2,1,250,64]{2,3,1,0:T(8,128)S(1)} %pad_maximum_fusion), channel_id=1, replica_groups=mesh['grp'=2,'row_0'=8,'row_1'=2,'col'=8] {'row_1'}, dimensions={0} | all-to-all | bytes 256000 | tf_op jit(solution)/shard_map/all_to_all | solution.py:13
  193.8 0.1 copy.30
  193.9 1.2 stack.7
  195.2 7.3 %all-to-all-start.3 = ((f32[8,2,250,64]{2,1,3,0:T(2,128)}), f32[8,2,250,64]{2,1,3,0:T(2,128)}, u32[]{:S(2)}, u32[]{:S(2)}) async-start(f32[8,2,250,64]{2,1,3,0:T(2,128)} %stack.7), calls=%async_computation.5 | async-start | bytes 2097152 | tf_op jit(solution)/shard_map/all_to_all | solution.py:13
  202.4 0.8 dynamic_slice.3
  203.2 0.0 copy-done.2
  203.2 0.9 broadcast_subtract_fusion
  204.1 24.9 %all-to-all-done.3 = f32[8,2,250,64]{2,1,3,0:T(2,128)} async-done(((f32[8,2,250,64]{2,1,3,0:T(2,128)}), f32[8,2,250,64]{2,1,3,0:T(2,128)}, u32[]{:S(2)}, u32[]{:S(2)}) %all-to-all-start.3) | async-done | bytes 1024032 | tf_op jit(solution)/shard_map/all_to_all | solution.py:13
  228.9 2.8 copy.31
  231.7 4.3 %reshape_reshape_reshape_reshape_reshape.3 = f32[2,2000,64]{1,0,2:T(2,128)} reshape(f32[8,2,250,64]{2,1,0,3:T(2,128)} %copy.31) | data formatting | bytes 2048000 | tf_op jit(solution)/shard_map/reshape;reshape;reshape;reshape;reshape | solution.py:72
  236.1 1.9 divide_convert_fusion
  238.0 1.1 fusion.15
  239.1 0.1 broadcast_in_dim.10
  239.2 0.0 copy-start.1
  239.2 43.8 %all_to_all.26 = bf16[8,2,750,64]{2,3,1,0:T(8,128)(2,1)S(1)} all-to-all(bf16[8,2,750,64]{2,3,1,0:T(8,128)(2,1)S(1)} %broadcast_in_dim.10), channel_id=1, replica_groups=mesh['grp'=2,'row_0'=8,'row_1'=2,'col'=8] {'col'}, dimensions={0} | all-to-all | bytes 3072000 | tf_op jit(solution)/shard_map/all_to_all | solution.py:25
  283.0 0.1 copy.34
  283.1 0.0 copy-done.1
  283.1 4.7 %convolution_convert_fusion = bf16[2,750,1500]{2,1,0:T(8,128)(2,1)} fusion(bf16[2,750,512]{1,2,0:T(8,128)(2,1)S(1)} %bitcast.44, bf16[1500,512,1]{0,1,2:T(8,128)(2,1)S(1)} %bitcast.43), kind=kOutput, calls=%fused_computation.2 | convolution fusion | flops 2306249984 | bytes 7572000 | tf_op jit(solution)/shard_map/piv,jv->pij/dot_general | solution.py:97
  287.8 9.2 %copy.37 = bf16[2,750,1500]{2,0,1:T(2,128)(2,1)} copy(bf16[2,750,1500]{2,1,0:T(8,128)(2,1)} %convolution_convert_fusion) | data formatting | bytes 9000000 | tf_op jit(solution)/shard_map/convert_element_type | solution.py:100
Async XLA Ops:
  8.7 58.7 %all-to-all-start = ((bf16[16,1500,32]{1,2,0:T(8,128)(2,1)}), bf16[16,1500,32]{1,2,0:T(8,128)(2,1)S(1)}, u32[]{:S(2)}, u32[]{:S(2)}) async-start(bf16[16,1500,32]{1,2,0:T(8,128)(2,1)} %broadcast_in_dim.4), calls=%async_computation | async-start | bytes 3145728 | tf_op jit(solution)/shard_map/all_to_all | solution.py:25
  31.5 50.8 %all-gather.3.cloned.1.call-start = ((), (), s32[]{:S(2)}) async-start(), calls=%async_computation.9 | async-start | bytes 3465216 | tf_op jit(solution)/shard_map/all_gather | solution.py:76
  67.4 1.2 copy-start
  77.7 45.8 %all-to-all-start.1 = ((bf16[8,64,2,750]{3,1,2,0:T(8,128)(2,1)}), bf16[8,64,2,750]{3,1,2,0:T(8,128)(2,1)}, u32[]{:S(2)}, u32[]{:S(2)}) async-start(bf16[8,64,2,750]{3,1,2,0:T(8,128)(2,1)} %copy.25), calls=%async_computation.1 | async-start | bytes 3145728 | tf_op jit(solution)/shard_map/all_to_all | solution.py:39
  82.2 89.7 %reduce-scatter.3.cloned.1.call-start = ((), (), s32[]{:S(2)}) async-start(), calls=%async_computation.7 | async-start | bytes 1179648 | tf_op jit(solution)/shard_map/reduce_scatter | solution.py:53
  134.7 68.5 %copy-start.2 = (f32[2000]{0:T(1024)S(1)}, f32[2000]{0:T(1024)}, u32[]{:S(2)}) copy-start(f32[2000]{0:T(1024)} %param.8) | copy-start | bytes 24004
  134.7 54.3 %reduce-scatter.5.cloned.1.call-start = ((), (), s32[]{:S(2)}) async-start(), calls=%async_computation.8 | async-start | bytes 196608 | tf_op jit(solution)/shard_map/reduce_scatter | solution.py:53
  195.2 33.8 %all-to-all-start.3 = ((f32[8,2,250,64]{2,1,3,0:T(2,128)}), f32[8,2,250,64]{2,1,3,0:T(2,128)}, u32[]{:S(2)}, u32[]{:S(2)}) async-start(f32[8,2,250,64]{2,1,3,0:T(2,128)} %stack.7), calls=%async_computation.5 | async-start | bytes 2097152 | tf_op jit(solution)/shard_map/all_to_all | solution.py:13
  239.2 43.9 %copy-start.1 = (bf16[16,1500,32]{1,2,0:T(8,128)(2,1)S(1)}, bf16[16,1500,32]{1,2,0:T(8,128)(2,1)}, u32[]{:S(2)}) copy-start(bf16[16,1500,32]{1,2,0:T(8,128)(2,1)} %copy-done) | copy-start | bytes 4608004
Sparse Core Ops, SparseCore 0:
  34.2 48.1 all-gather.2
  134.9 36.9 reduce-scatter.2
  174.3 14.6 reduce-scatter.4
